TPU v7x, 512 devices: a 8x2x16 block of a 8x8x16 slice. The times are simulated.
512 devices in a mesh: grp: 2 (over y), src: 16 (over z), rcv: 8 (over x), frq: 2 (over core).
Axes of the slice: x: 8, y: 2, z: 16, core: 2. Of those that a mesh axis runs over, the one named last changes fastest.
The devices are a block of a 8x8x16 slice.
Arguments:
- left_strip: bfloat16 [4, 2, 1024, 20480], P(('grp', 'frq'), None, 'src', 'rcv'), parts along dimension 0, may hold values from -0.03125 to 0.03125
- right_strip: bfloat16 [4, 2, 1536, 20480], P(('grp', 'frq'), None, 'src', 'rcv'), parts along dimension 0, may hold values from -6 to 6
- panel_order: int32 [40], P('rcv'), may hold values from 0 to 39, as said below
- freq_slice: int32 [4], P(('grp', 'frq')), parts along dimension 0, may hold values from 0 to 63
- wavelet: float32 [64, 2], replicated, may hold values from -4 to 4
Outputs:
- multiple: float32 [4, 2, 1536, 1024], P(('grp', 'frq'), None, 'src', 'rcv'), parts along dimension 0
There are 2 independent parts, one for each index of `grp`. A program takes and returns all parts, laid end to end along the dimension named above; an argument that names none is the same for every part. Nothing has to cross between parts.
Inputs may be any that keep to these rules, and one draw needn't show every extreme that they name: `panel_order`: each aligned block of 5 entries is a permutation of that block's own positions.
All inputs are finite; a program needn't handle non-finite values.
Results may differ from a plain program's by a relative error of at most 0.0003.
Values may be sent and summed in bfloat16 or wider, within the bound.
No kernel may reach another device: no remote copies, remote signals or barrier semaphores. Data moves between devices by JAX's collectives and lax.ppermute only.
A program may use at most 64 MiB of HBM per device.

v0:
```python
import functools

import jax
import jax.numpy as jnp
from jax import lax
from jax.experimental import pallas as pl
from jax.experimental.pallas import tpu as pltpu
from jax.sharding import PartitionSpec as P


CHUNKS = 2
PRODUCT_STEPS = (3, 6)
PRODUCT_VMEM = 24 << 20
SMALL_VMEM = 8 << 20
VMEM = pltpu.VMEM
SMEM = pltpu.SMEM


def order_kernel(order, right, out):
    panels = order.shape[0]
    sources, positions = right.shape[2], right.shape[3]
    width = positions // panels
    for p in range(panels):
        target = pl.multiple_of(lax.rem(order[p], panels) * width, width)
        for part in range(2):
            out[pl.ds(part * sources, sources), pl.ds(target, width)] = right[
                0, part, :, pl.ds(p * width, width)
            ]


def multiply(right, refs):
    rows = refs[0].shape[1] * CHUNKS
    sources = right.shape[0] // 2

    def with_part(part):
        left = jnp.concatenate([ref[part] for ref in refs], axis=0)
        return lax.dot_general(
            right[...], left, (((1,), (1,)), ((), ())), preferred_element_type=jnp.float32
        )

    by_real, by_imag = with_part(0), with_part(1)
    real = by_real[:sources] - by_imag[sources:]
    imag = by_imag[:sources] + by_real[sources:]
    return [
        jnp.concatenate(
            [real[:, i * rows : (i + 1) * rows], imag[:, i * rows : (i + 1) * rows]], axis=1
        )
        for i in range(len(refs) // CHUNKS)
    ]


def product_kernel(right, *refs):
    for i, piece in enumerate(multiply(right, refs[:-1])):
        refs[-1][i] = piece


def flat(held):
    return [chunk for block in held.values() for chunk in block]


def product(right, held):
    rows = sum(chunk.shape[1] for chunk in next(iter(held.values())))
    operands = [right, *flat(held)]
    return pl.pallas_call(
        product_kernel,
        out_shape=jax.ShapeDtypeStruct((len(held), right.shape[0] // 2, 2 * rows), jnp.float32),
        in_specs=[pl.BlockSpec(memory_space=VMEM)] * len(operands),
        out_specs=pl.BlockSpec(memory_space=VMEM),
        compiler_params=pltpu.CompilerParams(vmem_limit_bytes=PRODUCT_VMEM),
        name="product",
    )(*operands)


def assemble_kernel(early, late, n, per, place, right, *refs):
    out = refs[-1]

    def store(r, piece):
        lanes = piece.shape[1]
        out[lax.rem(place[0] + r, n) // per, :, pl.ds((r % per) * lanes, lanes)] = piece

    for relative, pieces in zip(early, refs):
        for i, r in enumerate(relative):
            store(r, pieces[i])
    for r, piece in zip(late, multiply(right, refs[len(early) : -1])):
        store(r, piece)


def assemble(place, right, early, pieces, held, n, m):
    lanes = pieces[0].shape[2]
    per = n // m
    operands = [right, *pieces, *flat(held)]
    return pl.pallas_call(
        functools.partial(assemble_kernel, early, tuple(held), n, per),
        out_shape=jax.ShapeDtypeStruct((m, right.shape[0] // 2, per * lanes), jnp.float32),
        in_specs=[pl.BlockSpec(memory_space=SMEM)]
        + [pl.BlockSpec(memory_space=VMEM)] * len(operands),
        out_specs=pl.BlockSpec(memory_space=VMEM),
        compiler_params=pltpu.CompilerParams(vmem_limit_bytes=PRODUCT_VMEM),
        name="assemble",
    )(place, *operands)


def finish_kernel(place, slice_of, wavelet, *refs):
    arrived, out = refs[:-1], refs[-1]
    lanes = arrived[0].shape[2]
    rows = lanes // 4
    odd = lax.rem(place[0], 2) == 1
    sums = [ref[...].sum(axis=0) for ref in arrived]

    def lay(part):
        halves = [
            jnp.concatenate(
                [s[:, (2 * h + part) * rows : (2 * h + part + 1) * rows] for s in sums], axis=1
            )
            for h in range(2)
        ]
        return jnp.concatenate(
            [jnp.where(odd, halves[1], halves[0]), jnp.where(odd, halves[0], halves[1])], axis=1
        )

    real, imag = lay(0), lay(1)
    index = slice_of[0]
    weight_real, weight_imag = wavelet[0, index], wavelet[1, index]
    out[0, 0] = weight_real * real - weight_imag * imag
    out[0, 1] = weight_real * imag + weight_imag * real


def local(left_strip, right_strip, panel_order, freq_slice, wavelet):
    _, _, receivers, positions = left_strip.shape
    sources = right_strip.shape[2]
    n, m = lax.axis_size("src"), lax.axis_size("rcv")
    place = lax.axis_index("src").astype(jnp.int32).reshape(1)
    right = pl.pallas_call(
        order_kernel,
        out_shape=jax.ShapeDtypeStruct((2 * sources, positions), jnp.bfloat16),
        in_specs=[
            pl.BlockSpec(memory_space=SMEM),
            pl.BlockSpec(memory_space=VMEM),
        ],
        out_specs=pl.BlockSpec(memory_space=VMEM),
        compiler_params=pltpu.CompilerParams(vmem_limit_bytes=SMALL_VMEM),
        name="order",
    )(panel_order, right_strip)
    up = [(i, (i + 1) % n) for i in range(n)]
    down = [(i, (i - 1) % n) for i in range(n)]
    half = n // 2
    rows = receivers // CHUNKS
    own = [left_strip[0, :, c * rows : (c + 1) * rows] for c in range(CHUNKS)]
    above, below = list(own), list(own)
    held = {0: tuple(own)}
    pieces, early = [], []
    for step in range(1, half + 1):
        if step in PRODUCT_STEPS:
            pieces.append(product(right, held))
            early.append(tuple(held))
            held = {}
        for c in range(CHUNKS):
            above[c] = lax.ppermute(above[c], "src", down)
            if step < half:
                below[c] = lax.ppermute(below[c], "src", up)
        held[step] = tuple(above)
        if step < half:
            held[n - step] = tuple(below)
    tiles = assemble(place, right, early, pieces, held, n, m)
    arrived = [lax.all_to_all(tiles, "rcv", split_axis=0, concat_axis=0, tiled=True)]
    return pl.pallas_call(
        finish_kernel,
        out_shape=jax.ShapeDtypeStruct((1, 2, sources, n * receivers // m), jnp.float32),
        in_specs=[pl.BlockSpec(memory_space=SMEM)] * 3 + [pl.BlockSpec(memory_space=VMEM)],
        out_specs=pl.BlockSpec(memory_space=VMEM),
        compiler_params=pltpu.CompilerParams(vmem_limit_bytes=SMALL_VMEM),
        name="finish",
    )(place, freq_slice, wavelet.T, *arrived)


def solution(mesh):
    placed = (
        P(("grp", "frq"), None, "src", "rcv"),
        P(("grp", "frq"), None, "src", "rcv"),
        P("rcv"),
        P(("grp", "frq")),
        P(),
    )
    return jax.shard_map(
        local,
        mesh=mesh,
        in_specs=placed,
        out_specs=P(("grp", "frq"), None, "src", "rcv"),
        check_vma=False,
    )
```

profile of v0, /device:TPU:80, one launch (start us, length us, event | category | flops | bytes accessed | tf_op | source)
XLA Modules:
  0.0 193.9 jit_solution(2914340135166078919)
XLA Ops:
  1.2 44.0 %collective-permute-start = (bf16[2,32,2560]{2,1,0:T(8,128)(2,1)S(1)}, bf16[2,32,2560]{2,1,0:T(8,128)(2,1)S(1)}, u32[]{:S(2)}, u32[]{:S(2)}) collective-permute-start(bf16[2,32,2560]{2,1,0:T(8,128)(2,1)S(1)} %get-tuple-element.6.refs_0_), channel_id=1, source_target_pairs={{0,240},{16,0},{32,16},{48,32},{64,48},{80,64},{96,80},{112,96},{1... | collective-permute-start | bytes 983048 | tf_op jit(solution)/shard_map/ppermute | solution.py:158
  47.2 4.0 %collective-permute-start.2 = (bf16[2,32,2560]{2,1,0:T(8,128)(2,1)S(1)}, bf16[2,32,2560]{2,1,0:T(8,128)(2,1)S(1)}, u32[]{:S(2)}, u32[]{:S(2)}) collective-permute-start(bf16[2,32,2560]{2,1,0:T(8,128)(2,1)S(1)} %get-tuple-element.6.refs_0_), channel_id=1, source_target_pairs={{0,16},{16,32},{32,48},{48,64},{64,80},{80,96},{96,112},{112,128},... | collective-permute-start | bytes 983048 | tf_op jit(solution)/shard_map/ppermute | solution.py:160
  53.3 5.6 %collective-permute-start.4 = (bf16[2,32,2560]{2,1,0:T(8,128)(2,1)S(1)}, bf16[2,32,2560]{2,1,0:T(8,128)(2,1)S(1)}, u32[]{:S(2)}, u32[]{:S(2)}) collective-permute-start(bf16[2,32,2560]{2,1,0:T(8,128)(2,1)S(1)} %collective-permute-done.refs_2_), channel_id=1, source_target_pairs={{0,240},{16,0},{32,16},{48,32},{64,48},{80,64},{96,80},{112,96},{1... | collective-permute-start | bytes 983048 | tf_op jit(solution)/shard_map/ppermute | solution.py:158
  60.3 5.6 %collective-permute-start.5 = (bf16[2,32,2560]{2,1,0:T(8,128)(2,1)S(1)}, bf16[2,32,2560]{2,1,0:T(8,128)(2,1)S(1)}, u32[]{:S(2)}, u32[]{:S(2)}) collective-permute-start(bf16[2,32,2560]{2,1,0:T(8,128)(2,1)S(1)} %collective-permute-done.1.refs_3_), channel_id=1, source_target_pairs={{0,240},{16,0},{32,16},{48,32},{64,48},{80,64},{96,80},{112,96},{1... | collective-permute-start | bytes 983048 | tf_op jit(solution)/shard_map/ppermute | solution.py:158
  69.9 5.2 %collective-permute-start.8 = (bf16[2,32,2560]{2,1,0:T(8,128)(2,1)S(1)}, bf16[2,32,2560]{2,1,0:T(8,128)(2,1)S(1)}, u32[]{:S(2)}, u32[]{:S(2)}) collective-permute-start(bf16[2,32,2560]{2,1,0:T(8,128)(2,1)S(1)} %collective-permute-done.4.refs_6_), channel_id=1, source_target_pairs={{0,240},{16,0},{32,16},{48,32},{64,48},{80,64},{96,80},{112,96},{1... | collective-permute-start | bytes 983048 | tf_op jit(solution)/shard_map/ppermute | solution.py:158
  75.1 4.6 %collective-permute-start.9 = (bf16[2,32,2560]{2,1,0:T(8,128)(2,1)S(1)}, bf16[2,32,2560]{2,1,0:T(8,128)(2,1)S(1)}, u32[]{:S(2)}, u32[]{:S(2)}) collective-permute-start(bf16[2,32,2560]{2,1,0:T(8,128)(2,1)S(1)} %collective-permute-done.5.refs_7_), channel_id=1, source_target_pairs={{0,240},{16,0},{32,16},{48,32},{64,48},{80,64},{96,80},{112,96},{1... | collective-permute-start | bytes 983048 | tf_op jit(solution)/shard_map/ppermute | solution.py:158
  86.1 5.2 %collective-permute-start.12 = (bf16[2,32,2560]{2,1,0:T(8,128)(2,1)S(1)}, bf16[2,32,2560]{2,1,0:T(8,128)(2,1)S(1)}, u32[]{:S(2)}, u32[]{:S(2)}) collective-permute-start(bf16[2,32,2560]{2,1,0:T(8,128)(2,1)S(1)} %collective-permute-done.8.refs_0_), channel_id=1, source_target_pairs={{0,240},{16,0},{32,16},{48,32},{64,48},{80,64},{96,80},{112,96},{1... | collective-permute-start | bytes 983048 | tf_op jit(solution)/shard_map/ppermute | solution.py:158
  92.0 3.6 %collective-permute-start.13 = (bf16[2,32,2560]{2,1,0:T(8,128)(2,1)S(1)}, bf16[2,32,2560]{2,1,0:T(8,128)(2,1)S(1)}, u32[]{:S(2)}, u32[]{:S(2)}) collective-permute-start(bf16[2,32,2560]{2,1,0:T(8,128)(2,1)S(1)} %collective-permute-done.9.refs_1_), channel_id=1, source_target_pairs={{0,240},{16,0},{32,16},{48,32},{64,48},{80,64},{96,80},{112,96},{1... | collective-permute-start | bytes 983048 | tf_op jit(solution)/shard_map/ppermute | solution.py:158
  96.4 2.3 %collective-permute-start.14 = (bf16[2,32,2560]{2,1,0:T(8,128)(2,1)S(1)}, bf16[2,32,2560]{2,1,0:T(8,128)(2,1)S(1)}, u32[]{:S(2)}, u32[]{:S(2)}) collective-permute-start(bf16[2,32,2560]{2,1,0:T(8,128)(2,1)S(1)} %collective-permute-done.10.refs_2_), channel_id=1, source_target_pairs={{0,16},{16,32},{32,48},{48,64},{64,80},{80,96},{96,112},{112,128},... | collective-permute-start | bytes 983048 | tf_op jit(solution)/shard_map/ppermute | solution.py:160
  102.1 5.2 %collective-permute-start.16 = (bf16[2,32,2560]{2,1,0:T(8,128)(2,1)S(1)}, bf16[2,32,2560]{2,1,0:T(8,128)(2,1)S(1)}, u32[]{:S(2)}, u32[]{:S(2)}) collective-permute-start(bf16[2,32,2560]{2,1,0:T(8,128)(2,1)S(1)} %collective-permute-done.12.refs_4_), channel_id=1, source_target_pairs={{0,240},{16,0},{32,16},{48,32},{64,48},{80,64},{96,80},{112,96},{1... | collective-permute-start | bytes 983048 | tf_op jit(solution)/shard_map/ppermute | solution.py:158
  108.0 3.6 %collective-permute-start.17 = (bf16[2,32,2560]{2,1,0:T(8,128)(2,1)S(1)}, bf16[2,32,2560]{2,1,0:T(8,128)(2,1)S(1)}, u32[]{:S(2)}, u32[]{:S(2)}) collective-permute-start(bf16[2,32,2560]{2,1,0:T(8,128)(2,1)S(1)} %collective-permute-done.13.refs_5_), channel_id=1, source_target_pairs={{0,240},{16,0},{32,16},{48,32},{64,48},{80,64},{96,80},{112,96},{1... | collective-permute-start | bytes 983048 | tf_op jit(solution)/shard_map/ppermute | solution.py:158
  112.3 2.3 %collective-permute-start.18 = (bf16[2,32,2560]{2,1,0:T(8,128)(2,1)S(1)}, bf16[2,32,2560]{2,1,0:T(8,128)(2,1)S(1)}, u32[]{:S(2)}, u32[]{:S(2)}) collective-permute-start(bf16[2,32,2560]{2,1,0:T(8,128)(2,1)S(1)} %collective-permute-done.14.refs_6_), channel_id=1, source_target_pairs={{0,16},{16,32},{32,48},{48,64},{64,80},{80,96},{96,112},{112,128},... | collective-permute-start | bytes 983048 | tf_op jit(solution)/shard_map/ppermute | solution.py:160
  118.1 5.2 %collective-permute-start.20 = (bf16[2,32,2560]{2,1,0:T(8,128)(2,1)S(1)}, bf16[2,32,2560]{2,1,0:T(8,128)(2,1)S(1)}, u32[]{:S(2)}, u32[]{:S(2)}) collective-permute-start(bf16[2,32,2560]{2,1,0:T(8,128)(2,1)S(1)} %collective-permute-done.16.refs_8_), channel_id=1, source_target_pairs={{0,240},{16,0},{32,16},{48,32},{64,48},{80,64},{96,80},{112,96},{1... | collective-permute-start | bytes 983048 | tf_op jit(solution)/shard_map/ppermute | solution.py:158
  123.9 3.6 %collective-permute-start.21 = (bf16[2,32,2560]{2,1,0:T(8,128)(2,1)S(1)}, bf16[2,32,2560]{2,1,0:T(8,128)(2,1)S(1)}, u32[]{:S(2)}, u32[]{:S(2)}) collective-permute-start(bf16[2,32,2560]{2,1,0:T(8,128)(2,1)S(1)} %collective-permute-done.17.refs_9_), channel_id=1, source_target_pairs={{0,240},{16,0},{32,16},{48,32},{64,48},{80,64},{96,80},{112,96},{1... | collective-permute-start | bytes 983048 | tf_op jit(solution)/shard_map/ppermute | solution.py:158
  128.2 2.3 %collective-permute-start.22 = (bf16[2,32,2560]{2,1,0:T(8,128)(2,1)S(1)}, bf16[2,32,2560]{2,1,0:T(8,128)(2,1)}, u32[]{:S(2)}, u32[]{:S(2)}) collective-permute-start(bf16[2,32,2560]{2,1,0:T(8,128)(2,1)S(1)} %collective-permute-done.18.refs_10_), channel_id=1, source_target_pairs={{0,16},{16,32},{32,48},{48,64},{64,80},{80,96},{96,112},{112,128},... | collective-permute-start | bytes 983048 | tf_op jit(solution)/shard_map/ppermute | solution.py:160
  134.0 5.2 %collective-permute-start.24 = (bf16[2,32,2560]{2,1,0:T(8,128)(2,1)S(1)}, bf16[2,32,2560]{2,1,0:T(8,128)(2,1)}, u32[]{:S(2)}, u32[]{:S(2)}) collective-permute-start(bf16[2,32,2560]{2,1,0:T(8,128)(2,1)S(1)} %collective-permute-done.20.refs_2_), channel_id=1, source_target_pairs={{0,240},{16,0},{32,16},{48,32},{64,48},{80,64},{96,80},{112,96},{1... | collective-permute-start | bytes 983048 | tf_op jit(solution)/shard_map/ppermute | solution.py:158
  139.9 3.6 %collective-permute-start.25 = (bf16[2,32,2560]{2,1,0:T(8,128)(2,1)S(1)}, bf16[2,32,2560]{2,1,0:T(8,128)(2,1)}, u32[]{:S(2)}, u32[]{:S(2)}) collective-permute-start(bf16[2,32,2560]{2,1,0:T(8,128)(2,1)S(1)} %collective-permute-done.21.refs_3_), channel_id=1, source_target_pairs={{0,240},{16,0},{32,16},{48,32},{64,48},{80,64},{96,80},{112,96},{1... | collective-permute-start | bytes 983048 | tf_op jit(solution)/shard_map/ppermute | solution.py:158
  144.3 2.3 %collective-permute-start.26 = (bf16[2,32,2560]{2,1,0:T(8,128)(2,1)}, bf16[2,32,2560]{2,1,0:T(8,128)(2,1)}, u32[]{:S(2)}, u32[]{:S(2)}) collective-permute-start(bf16[2,32,2560]{2,1,0:T(8,128)(2,1)} %collective-permute-done.22.refs_4_), channel_id=1, source_target_pairs={{0,16},{16,32},{32,48},{48,64},{64,80},{80,96},{96,112},{112,128},... | collective-permute-start | bytes 983048 | tf_op jit(solution)/shard_map/ppermute | solution.py:160
  146.6 2.0 %collective-permute-start.27 = (bf16[2,32,2560]{2,1,0:T(8,128)(2,1)}, bf16[2,32,2560]{2,1,0:T(8,128)(2,1)}, u32[]{:S(2)}, u32[]{:S(2)}) collective-permute-start(bf16[2,32,2560]{2,1,0:T(8,128)(2,1)} %collective-permute-done.23.refs_5_), channel_id=1, source_target_pairs={{0,16},{16,32},{32,48},{48,64},{64,80},{80,96},{96,112},{112,128},... | collective-permute-start | bytes 983048 | tf_op jit(solution)/shard_map/ppermute | solution.py:160
  148.6 5.2 %collective-permute-start.28 = (bf16[2,32,2560]{2,1,0:T(8,128)(2,1)}, bf16[2,32,2560]{2,1,0:T(8,128)(2,1)}, u32[]{:S(2)}, u32[]{:S(2)}) collective-permute-start(bf16[2,32,2560]{2,1,0:T(8,128)(2,1)} %collective-permute-done.24.refs_6_), channel_id=1, source_target_pairs={{0,240},{16,0},{32,16},{48,32},{64,48},{80,64},{96,80},{112,96},{1... | collective-permute-start | bytes 983048 | tf_op jit(solution)/shard_map/ppermute | solution.py:158
  153.8 3.6 %collective-permute-start.29 = (bf16[2,32,2560]{2,1,0:T(8,128)(2,1)}, bf16[2,32,2560]{2,1,0:T(8,128)(2,1)}, u32[]{:S(2)}, u32[]{:S(2)}) collective-permute-start(bf16[2,32,2560]{2,1,0:T(8,128)(2,1)} %collective-permute-done.25.refs_7_), channel_id=1, source_target_pairs={{0,240},{16,0},{32,16},{48,32},{64,48},{80,64},{96,80},{112,96},{1... | collective-permute-start | bytes 983048 | tf_op jit(solution)/shard_map/ppermute | solution.py:158
  163.1 4.1 %assemble.1 = f32[8,96,256]{2,1,0:T(8,128)} custom-call(s32[1]{0:T(128)} %bitcast.place, bf16[192,2560]{1,0:T(8,128)(2,1)S(1)} %order.2.right, f32[5,96,128]{2,1,0:T(8,128)S(1)} %product.2.refs_0_, f32[6,96,128]{2,1,0:T(8,128)S(1)} %product.3.refs_1_, bf16[2,32,2560]{2,1,0:T(8,128)(2,1)S(1)} %copy-done.28, bf16[2,32,2560]{2,1,0:T(8,128)(2,1)S(1)} %copy-done.32, ...), custom_call_target="tpu_custom_call" | custom-call | tf_op jit(solution)/shard_map/assemble/pallas_call | solution.py:92
  167.2 7.3 %all-to-all-start = ((f32[8,96,256]{2,1,0:T(8,128)}), f32[8,96,256]{2,1,0:T(8,128)S(1)}, u32[]{:S(2)}, u32[]{:S(2)}) async-start(f32[8,96,256]{2,1,0:T(8,128)} %assemble.1), calls=%async_computation | async-start | bytes 1572864 | tf_op jit(solution)/shard_map/all_to_all | solution.py:165
  175.1 17.4 %all-to-all-done.refs_0_ = f32[8,96,256]{2,1,0:T(8,128)S(1)} async-done(((f32[8,96,256]{2,1,0:T(8,128)}), f32[8,96,256]{2,1,0:T(8,128)S(1)}, u32[]{:S(2)}, u32[]{:S(2)}) %all-to-all-start) | async-done | bytes 786464 | tf_op jit(solution)/shard_map/all_to_all | solution.py:165
  (118 shorter events, 40.0 us)
Async XLA Ops:
  1.2 52.1 %collective-permute-start = (bf16[2,32,2560]{2,1,0:T(8,128)(2,1)S(1)}, bf16[2,32,2560]{2,1,0:T(8,128)(2,1)S(1)}, u32[]{:S(2)}, u32[]{:S(2)}) collective-permute-start(bf16[2,32,2560]{2,1,0:T(8,128)(2,1)S(1)} %get-tuple-element.6.refs_0_), channel_id=1, source_target_pairs={{0,240},{16,0},{32,16},{48,32},{64,48},{80,64},{96,80},{112,96},{1... | collective-permute-start | bytes 983048 | tf_op jit(solution)/shard_map/ppermute | solution.py:158
  47.2 18.8 %collective-permute-start.2 = (bf16[2,32,2560]{2,1,0:T(8,128)(2,1)S(1)}, bf16[2,32,2560]{2,1,0:T(8,128)(2,1)S(1)}, u32[]{:S(2)}, u32[]{:S(2)}) collective-permute-start(bf16[2,32,2560]{2,1,0:T(8,128)(2,1)S(1)} %get-tuple-element.6.refs_0_), channel_id=1, source_target_pairs={{0,16},{16,32},{32,48},{48,64},{64,80},{80,96},{96,112},{112,128},... | collective-permute-start | bytes 983048 | tf_op jit(solution)/shard_map/ppermute | solution.py:160
  51.2 16.8 %collective-permute-start.3 = (bf16[2,32,2560]{2,1,0:T(8,128)(2,1)S(1)}, bf16[2,32,2560]{2,1,0:T(8,128)(2,1)S(1)}, u32[]{:S(2)}, u32[]{:S(2)}) collective-permute-start(bf16[2,32,2560]{2,1,0:T(8,128)(2,1)S(1)} %get-tuple-element.5.refs_1_), channel_id=1, source_target_pairs={{0,16},{16,32},{32,48},{48,64},{64,80},{80,96},{96,112},{112,128},... | collective-permute-start | bytes 983048 | tf_op jit(solution)/shard_map/ppermute | solution.py:160
  53.3 16.6 %collective-permute-start.4 = (bf16[2,32,2560]{2,1,0:T(8,128)(2,1)S(1)}, bf16[2,32,2560]{2,1,0:T(8,128)(2,1)S(1)}, u32[]{:S(2)}, u32[]{:S(2)}) collective-permute-start(bf16[2,32,2560]{2,1,0:T(8,128)(2,1)S(1)} %collective-permute-done.refs_2_), channel_id=1, source_target_pairs={{0,240},{16,0},{32,16},{48,32},{64,48},{80,64},{96,80},{112,96},{1... | collective-permute-start | bytes 983048 | tf_op jit(solution)/shard_map/ppermute | solution.py:158
  67.9 15.5 %collective-permute-start.7 = (bf16[2,32,2560]{2,1,0:T(8,128)(2,1)S(1)}, bf16[2,32,2560]{2,1,0:T(8,128)(2,1)S(1)}, u32[]{:S(2)}, u32[]{:S(2)}) collective-permute-start(bf16[2,32,2560]{2,1,0:T(8,128)(2,1)S(1)} %collective-permute-done.3.refs_5_), channel_id=1, source_target_pairs={{0,16},{16,32},{32,48},{48,64},{64,80},{80,96},{96,112},{112,128},... | collective-permute-start | bytes 983048 | tf_op jit(solution)/shard_map/ppermute | solution.py:160
  69.9 16.2 %collective-permute-start.8 = (bf16[2,32,2560]{2,1,0:T(8,128)(2,1)S(1)}, bf16[2,32,2560]{2,1,0:T(8,128)(2,1)S(1)}, u32[]{:S(2)}, u32[]{:S(2)}) collective-permute-start(bf16[2,32,2560]{2,1,0:T(8,128)(2,1)S(1)} %collective-permute-done.4.refs_6_), channel_id=1, source_target_pairs={{0,240},{16,0},{32,16},{48,32},{64,48},{80,64},{96,80},{112,96},{1... | collective-permute-start | bytes 983048 | tf_op jit(solution)/shard_map/ppermute | solution.py:158
  75.1 16.9 %collective-permute-start.9 = (bf16[2,32,2560]{2,1,0:T(8,128)(2,1)S(1)}, bf16[2,32,2560]{2,1,0:T(8,128)(2,1)S(1)}, u32[]{:S(2)}, u32[]{:S(2)}) collective-permute-start(bf16[2,32,2560]{2,1,0:T(8,128)(2,1)S(1)} %collective-permute-done.5.refs_7_), channel_id=1, source_target_pairs={{0,240},{16,0},{32,16},{48,32},{64,48},{80,64},{96,80},{112,96},{1... | collective-permute-start | bytes 983048 | tf_op jit(solution)/shard_map/ppermute | solution.py:158
  80.4 15.9 %collective-permute-start.10 = (bf16[2,32,2560]{2,1,0:T(8,128)(2,1)S(1)}, bf16[2,32,2560]{2,1,0:T(8,128)(2,1)S(1)}, u32[]{:S(2)}, u32[]{:S(2)}) collective-permute-start(bf16[2,32,2560]{2,1,0:T(8,128)(2,1)S(1)} %collective-permute-done.6.refs_8_), channel_id=1, source_target_pairs={{0,16},{16,32},{32,48},{48,64},{64,80},{80,96},{96,112},{112,128},... | collective-permute-start | bytes 983048 | tf_op jit(solution)/shard_map/ppermute | solution.py:160
  83.5 16.0 %collective-permute-start.11 = (bf16[2,32,2560]{2,1,0:T(8,128)(2,1)S(1)}, bf16[2,32,2560]{2,1,0:T(8,128)(2,1)S(1)}, u32[]{:S(2)}, u32[]{:S(2)}) collective-permute-start(bf16[2,32,2560]{2,1,0:T(8,128)(2,1)S(1)} %collective-permute-done.7.refs_9_), channel_id=1, source_target_pairs={{0,16},{16,32},{32,48},{48,64},{64,80},{80,96},{96,112},{112,128},... | collective-permute-start | bytes 983048 | tf_op jit(solution)/shard_map/ppermute | solution.py:160
  86.1 16.0 %collective-permute-start.12 = (bf16[2,32,2560]{2,1,0:T(8,128)(2,1)S(1)}, bf16[2,32,2560]{2,1,0:T(8,128)(2,1)S(1)}, u32[]{:S(2)}, u32[]{:S(2)}) collective-permute-start(bf16[2,32,2560]{2,1,0:T(8,128)(2,1)S(1)} %collective-permute-done.8.refs_0_), channel_id=1, source_target_pairs={{0,240},{16,0},{32,16},{48,32},{64,48},{80,64},{96,80},{112,96},{1... | collective-permute-start | bytes 983048 | tf_op jit(solution)/shard_map/ppermute | solution.py:158
  92.0 16.0 %collective-permute-start.13 = (bf16[2,32,2560]{2,1,0:T(8,128)(2,1)S(1)}, bf16[2,32,2560]{2,1,0:T(8,128)(2,1)S(1)}, u32[]{:S(2)}, u32[]{:S(2)}) collective-permute-start(bf16[2,32,2560]{2,1,0:T(8,128)(2,1)S(1)} %collective-permute-done.9.refs_1_), channel_id=1, source_target_pairs={{0,240},{16,0},{32,16},{48,32},{64,48},{80,64},{96,80},{112,96},{1... | collective-permute-start | bytes 983048 | tf_op jit(solution)/shard_map/ppermute | solution.py:158
  96.4 16.0 %collective-permute-start.14 = (bf16[2,32,2560]{2,1,0:T(8,128)(2,1)S(1)}, bf16[2,32,2560]{2,1,0:T(8,128)(2,1)S(1)}, u32[]{:S(2)}, u32[]{:S(2)}) collective-permute-start(bf16[2,32,2560]{2,1,0:T(8,128)(2,1)S(1)} %collective-permute-done.10.refs_2_), channel_id=1, source_target_pairs={{0,16},{16,32},{32,48},{48,64},{64,80},{80,96},{96,112},{112,128},... | collective-permute-start | bytes 983048 | tf_op jit(solution)/shard_map/ppermute | solution.py:160
  99.4 15.9 %collective-permute-start.15 = (bf16[2,32,2560]{2,1,0:T(8,128)(2,1)S(1)}, bf16[2,32,2560]{2,1,0:T(8,128)(2,1)S(1)}, u32[]{:S(2)}, u32[]{:S(2)}) collective-permute-start(bf16[2,32,2560]{2,1,0:T(8,128)(2,1)S(1)} %collective-permute-done.11.refs_3_), channel_id=1, source_target_pairs={{0,16},{16,32},{32,48},{48,64},{64,80},{80,96},{96,112},{112,128},... | collective-permute-start | bytes 983048 | tf_op jit(solution)/shard_map/ppermute | solution.py:160
  102.1 15.9 %collective-permute-start.16 = (bf16[2,32,2560]{2,1,0:T(8,128)(2,1)S(1)}, bf16[2,32,2560]{2,1,0:T(8,128)(2,1)S(1)}, u32[]{:S(2)}, u32[]{:S(2)}) collective-permute-start(bf16[2,32,2560]{2,1,0:T(8,128)(2,1)S(1)} %collective-permute-done.12.refs_4_), channel_id=1, source_target_pairs={{0,240},{16,0},{32,16},{48,32},{64,48},{80,64},{96,80},{112,96},{1... | collective-permute-start | bytes 983048 | tf_op jit(solution)/shard_map/ppermute | solution.py:158
  108.0 15.9 %collective-permute-start.17 = (bf16[2,32,2560]{2,1,0:T(8,128)(2,1)S(1)}, bf16[2,32,2560]{2,1,0:T(8,128)(2,1)S(1)}, u32[]{:S(2)}, u32[]{:S(2)}) collective-permute-start(bf16[2,32,2560]{2,1,0:T(8,128)(2,1)S(1)} %collective-permute-done.13.refs_5_), channel_id=1, source_target_pairs={{0,240},{16,0},{32,16},{48,32},{64,48},{80,64},{96,80},{112,96},{1... | collective-permute-start | bytes 983048 | tf_op jit(solution)/shard_map/ppermute | solution.py:158
  112.3 15.9 %collective-permute-start.18 = (bf16[2,32,2560]{2,1,0:T(8,128)(2,1)S(1)}, bf16[2,32,2560]{2,1,0:T(8,128)(2,1)S(1)}, u32[]{:S(2)}, u32[]{:S(2)}) collective-permute-start(bf16[2,32,2560]{2,1,0:T(8,128)(2,1)S(1)} %collective-permute-done.14.refs_6_), channel_id=1, source_target_pairs={{0,16},{16,32},{32,48},{48,64},{64,80},{80,96},{96,112},{112,128},... | collective-permute-start | bytes 983048 | tf_op jit(solution)/shard_map/ppermute | solution.py:160
  115.4 16.0 %collective-permute-start.19 = (bf16[2,32,2560]{2,1,0:T(8,128)(2,1)S(1)}, bf16[2,32,2560]{2,1,0:T(8,128)(2,1)S(1)}, u32[]{:S(2)}, u32[]{:S(2)}) collective-permute-start(bf16[2,32,2560]{2,1,0:T(8,128)(2,1)S(1)} %collective-permute-done.15.refs_7_), channel_id=1, source_target_pairs={{0,16},{16,32},{32,48},{48,64},{64,80},{80,96},{96,112},{112,128},... | collective-permute-start | bytes 983048 | tf_op jit(solution)/shard_map/ppermute | solution.py:160
  118.1 16.0 %collective-permute-start.20 = (bf16[2,32,2560]{2,1,0:T(8,128)(2,1)S(1)}, bf16[2,32,2560]{2,1,0:T(8,128)(2,1)S(1)}, u32[]{:S(2)}, u32[]{:S(2)}) collective-permute-start(bf16[2,32,2560]{2,1,0:T(8,128)(2,1)S(1)} %collective-permute-done.16.refs_8_), channel_id=1, source_target_pairs={{0,240},{16,0},{32,16},{48,32},{64,48},{80,64},{96,80},{112,96},{1... | collective-permute-start | bytes 983048 | tf_op jit(solution)/shard_map/ppermute | solution.py:158
  123.9 16.0 %collective-permute-start.21 = (bf16[2,32,2560]{2,1,0:T(8,128)(2,1)S(1)}, bf16[2,32,2560]{2,1,0:T(8,128)(2,1)S(1)}, u32[]{:S(2)}, u32[]{:S(2)}) collective-permute-start(bf16[2,32,2560]{2,1,0:T(8,128)(2,1)S(1)} %collective-permute-done.17.refs_9_), channel_id=1, source_target_pairs={{0,240},{16,0},{32,16},{48,32},{64,48},{80,64},{96,80},{112,96},{1... | collective-permute-start | bytes 983048 | tf_op jit(solution)/shard_map/ppermute | solution.py:158
  128.2 16.0 %collective-permute-start.22 = (bf16[2,32,2560]{2,1,0:T(8,128)(2,1)S(1)}, bf16[2,32,2560]{2,1,0:T(8,128)(2,1)}, u32[]{:S(2)}, u32[]{:S(2)}) collective-permute-start(bf16[2,32,2560]{2,1,0:T(8,128)(2,1)S(1)} %collective-permute-done.18.refs_10_), channel_id=1, source_target_pairs={{0,16},{16,32},{32,48},{48,64},{64,80},{80,96},{96,112},{112,128},... | collective-permute-start | bytes 983048 | tf_op jit(solution)/shard_map/ppermute | solution.py:160
  131.3 15.3 %collective-permute-start.23 = (bf16[2,32,2560]{2,1,0:T(8,128)(2,1)S(1)}, bf16[2,32,2560]{2,1,0:T(8,128)(2,1)}, u32[]{:S(2)}, u32[]{:S(2)}) collective-permute-start(bf16[2,32,2560]{2,1,0:T(8,128)(2,1)S(1)} %collective-permute-done.19.refs_11_), channel_id=1, source_target_pairs={{0,16},{16,32},{32,48},{48,64},{64,80},{80,96},{96,112},{112,128},... | collective-permute-start | bytes 983048 | tf_op jit(solution)/shard_map/ppermute | solution.py:160
  144.3 18.5 %collective-permute-start.26 = (bf16[2,32,2560]{2,1,0:T(8,128)(2,1)}, bf16[2,32,2560]{2,1,0:T(8,128)(2,1)}, u32[]{:S(2)}, u32[]{:S(2)}) collective-permute-start(bf16[2,32,2560]{2,1,0:T(8,128)(2,1)} %collective-permute-done.22.refs_4_), channel_id=1, source_target_pairs={{0,16},{16,32},{32,48},{48,64},{64,80},{80,96},{96,112},{112,128},... | collective-permute-start | bytes 983048 | tf_op jit(solution)/shard_map/ppermute | solution.py:160
  146.6 16.2 %collective-permute-start.27 = (bf16[2,32,2560]{2,1,0:T(8,128)(2,1)}, bf16[2,32,2560]{2,1,0:T(8,128)(2,1)}, u32[]{:S(2)}, u32[]{:S(2)}) collective-permute-start(bf16[2,32,2560]{2,1,0:T(8,128)(2,1)} %collective-permute-done.23.refs_5_), channel_id=1, source_target_pairs={{0,16},{16,32},{32,48},{48,64},{64,80},{80,96},{96,112},{112,128},... | collective-permute-start | bytes 983048 | tf_op jit(solution)/shard_map/ppermute | solution.py:160
  167.2 25.4 %all-to-all-start = ((f32[8,96,256]{2,1,0:T(8,128)}), f32[8,96,256]{2,1,0:T(8,128)S(1)}, u32[]{:S(2)}, u32[]{:S(2)}) async-start(f32[8,96,256]{2,1,0:T(8,128)} %assemble.1), calls=%async_computation | async-start | bytes 1572864 | tf_op jit(solution)/shard_map/all_to_all | solution.py:165
  (44 other events, 311.5 us)
where the time goes:
time: 195 us; the launch traced here: 194 us
  starting transfers between devices  149 us (76%)
  waiting for transfers between devices  19.7 us (10%)
  local copies, waits for them, and re-layouts  15.2 us (8%)
  Pallas kernels  9.04 us (5%)
    ppermute x16, starting transfers between devices, local(): above[c] = lax.ppermute(above[c], 'src', down)  111 us
    ppermute x14, starting transfers between devices, local(): below[c] = lax.ppermute(below[c], 'src', up)  30.7 us
    all_to_all x1, waiting for transfers between devices, local(): lax.all_to_all(tiles, 'rcv', split_axis=0, concat_axis=0, tiled=True)  17.4 us
    unnamed x74, local copies, waits for them, and re-layouts  14 us
    all_to_all x1, starting transfers between devices, local(): lax.all_to_all(tiles, 'rcv', split_axis=0, concat_axis=0, tiled=True)  7.31 us
    pallas_call x1, Pallas kernels, assemble(): pl.pallas_call(functools.partial(assemble_kernel, early, tuple(held), n,...  4.08 us
  transfers between devices with their start and end apart: 31, of which 5 were waited for; matrix products, arithmetic and copies ran while one was open for 0% of the time, Pallas kernels for 2%

commit v1 on v0

--- a/solution.py
+++ b/solution.py
@@ -9,7 +9,7 @@
 
 
 CHUNKS = 2
-PRODUCT_STEPS = (3, 6)
+PRODUCT_STEPS = (3, 6, 8)
 PRODUCT_VMEM = 24 << 20
 SMALL_VMEM = 8 << 20
 VMEM = pltpu.VMEM
@@ -155,12 +155,15 @@
             early.append(tuple(held))
             held = {}
         for c in range(CHUNKS):
-            above[c] = lax.ppermute(above[c], "src", down)
-            if step < half:
+            if step < half or c == 0:
+                above[c] = lax.ppermute(above[c], "src", down)
+            if step < half or c == 1:
                 below[c] = lax.ppermute(below[c], "src", up)
-        held[step] = tuple(above)
         if step < half:
+            held[step] = tuple(above)
             held[n - step] = tuple(below)
+        else:
+            held[step] = (above[0], below[1])
     tiles = assemble(place, right, early, pieces, held, n, m)
     arrived = [lax.all_to_all(tiles, "rcv", split_axis=0, concat_axis=0, tiled=True)]
     return pl.pallas_call(

time: 195 us -> 197 us (1.010)
  starting transfers between devices: 149 us -> 153 us
  waiting for transfers between devices: 19.7 us -> 16.7 us
    ppermute x16 -> x15, starting transfers between devices: 111 us -> 116 us  [local(): above[c] = lax.ppermute(above[c], 'src', down)]
    pallas_call x2 -> x3, Pallas kernels: 3.03 us -> 5.58 us  [product(): pl.pallas_call(product_kernel, out_shape=jax.ShapeDtypeStruct((len(held),...]
    ppermute x14 -> x15, starting transfers between devices: 30.7 us -> 29.2 us  [local(): below[c] = lax.ppermute(below[c], 'src', up)]
  transfers between devices with their start and end apart: 31 -> 31, of which waited for: 5 -> 2; matrix products, arithmetic and copies ran while one was open for 0% -> 0% of each run, Pallas kernels for 2% -> 3%
where the time goes in v1:
time: 197 us; the launch traced here: 196 us
  starting transfers between devices  153 us (78%)
  waiting for transfers between devices  16.7 us (8%)
  local copies, waits for them, and re-layouts  15.1 us (8%)
  Pallas kernels  10.2 us (5%)
    ppermute x15, starting transfers between devices, local(): above[c] = lax.ppermute(above[c], 'src', down)  116 us
    ppermute x15, starting transfers between devices, local(): below[c] = lax.ppermute(below[c], 'src', up)  29.2 us
    all_to_all x1, waiting for transfers between devices, local(): lax.all_to_all(tiles, 'rcv', split_axis=0, concat_axis=0, tiled=True)  16.2 us
    unnamed x74, local copies, waits for them, and re-layouts  13.9 us
    all_to_all x1, starting transfers between devices, local(): lax.all_to_all(tiles, 'rcv', split_axis=0, concat_axis=0, tiled=True)  7.32 us
    pallas_call x3, Pallas kernels, product(): pl.pallas_call(product_kernel, out_shape=jax.ShapeDtypeStruct((len(held),...  5.58 us
  transfers between devices with their start and end apart: 31, of which 2 were waited for; matrix products, arithmetic and copies ran while one was open for 0% of the time, Pallas kernels for 3%

profile of v1, /device:TPU:80, one launch (start us, length us, event | category | flops | bytes accessed | tf_op | source)
XLA Modules:
  0.0 196.1 jit_solution(7043940271542229534)
XLA Ops:
  1.2 44.0 %collective-permute-start = (bf16[2,32,2560]{2,1,0:T(8,128)(2,1)S(1)}, bf16[2,32,2560]{2,1,0:T(8,128)(2,1)S(1)}, u32[]{:S(2)}, u32[]{:S(2)}) collective-permute-start(bf16[2,32,2560]{2,1,0:T(8,128)(2,1)S(1)} %get-tuple-element.6.refs_0_), channel_id=1, source_target_pairs={{0,240},{16,0},{32,16},{48,32},{64,48},{80,64},{96,80},{112,96},{1... | collective-permute-start | bytes 983048 | tf_op jit(solution)/shard_map/ppermute | solution.py:159
  45.2 2.0 collective-permute-start.3
  47.2 5.2 %collective-permute-start.1 = (bf16[2,32,2560]{2,1,0:T(8,128)(2,1)S(1)}, bf16[2,32,2560]{2,1,0:T(8,128)(2,1)S(1)}, u32[]{:S(2)}, u32[]{:S(2)}) collective-permute-start(bf16[2,32,2560]{2,1,0:T(8,128)(2,1)S(1)} %get-tuple-element.5.refs_1_), channel_id=1, source_target_pairs={{0,240},{16,0},{32,16},{48,32},{64,48},{80,64},{96,80},{112,96},{1... | collective-permute-start | bytes 983048 | tf_op jit(solution)/shard_map/ppermute | solution.py:159
  52.4 2.0 collective-permute-start.2
  54.3 5.2 %collective-permute-start.4 = (bf16[2,32,2560]{2,1,0:T(8,128)(2,1)S(1)}, bf16[2,32,2560]{2,1,0:T(8,128)(2,1)S(1)}, u32[]{:S(2)}, u32[]{:S(2)}) collective-permute-start(bf16[2,32,2560]{2,1,0:T(8,128)(2,1)S(1)} %collective-permute-done.refs_2_), channel_id=1, source_target_pairs={{0,240},{16,0},{32,16},{48,32},{64,48},{80,64},{96,80},{112,96},{1... | collective-permute-start | bytes 983048 | tf_op jit(solution)/shard_map/ppermute | solution.py:159
  61.5 5.2 %collective-permute-start.5 = (bf16[2,32,2560]{2,1,0:T(8,128)(2,1)S(1)}, bf16[2,32,2560]{2,1,0:T(8,128)(2,1)S(1)}, u32[]{:S(2)}, u32[]{:S(2)}) collective-permute-start(bf16[2,32,2560]{2,1,0:T(8,128)(2,1)S(1)} %collective-permute-done.1.refs_3_), channel_id=1, source_target_pairs={{0,240},{16,0},{32,16},{48,32},{64,48},{80,64},{96,80},{112,96},{1... | collective-permute-start | bytes 983048 | tf_op jit(solution)/shard_map/ppermute | solution.py:159
  66.7 2.0 collective-permute-start.6
  68.6 5.2 %collective-permute-start.8 = (bf16[2,32,2560]{2,1,0:T(8,128)(2,1)S(1)}, bf16[2,32,2560]{2,1,0:T(8,128)(2,1)S(1)}, u32[]{:S(2)}, u32[]{:S(2)}) collective-permute-start(bf16[2,32,2560]{2,1,0:T(8,128)(2,1)S(1)} %collective-permute-done.4.refs_6_), channel_id=1, source_target_pairs={{0,240},{16,0},{32,16},{48,32},{64,48},{80,64},{96,80},{112,96},{1... | collective-permute-start | bytes 983048 | tf_op jit(solution)/shard_map/ppermute | solution.py:159
  76.5 5.2 %collective-permute-start.9 = (bf16[2,32,2560]{2,1,0:T(8,128)(2,1)S(1)}, bf16[2,32,2560]{2,1,0:T(8,128)(2,1)S(1)}, u32[]{:S(2)}, u32[]{:S(2)}) collective-permute-start(bf16[2,32,2560]{2,1,0:T(8,128)(2,1)S(1)} %collective-permute-done.5.refs_7_), channel_id=1, source_target_pairs={{0,240},{16,0},{32,16},{48,32},{64,48},{80,64},{96,80},{112,96},{1... | collective-permute-start | bytes 983048 | tf_op jit(solution)/shard_map/ppermute | solution.py:159
  85.1 5.2 %collective-permute-start.12 = (bf16[2,32,2560]{2,1,0:T(8,128)(2,1)S(1)}, bf16[2,32,2560]{2,1,0:T(8,128)(2,1)S(1)}, u32[]{:S(2)}, u32[]{:S(2)}) collective-permute-start(bf16[2,32,2560]{2,1,0:T(8,128)(2,1)S(1)} %collective-permute-done.8.refs_0_), channel_id=1, source_target_pairs={{0,240},{16,0},{32,16},{48,32},{64,48},{80,64},{96,80},{112,96},{1... | collective-permute-start | bytes 983048 | tf_op jit(solution)/shard_map/ppermute | solution.py:159
  93.6 5.2 %collective-permute-start.13 = (bf16[2,32,2560]{2,1,0:T(8,128)(2,1)S(1)}, bf16[2,32,2560]{2,1,0:T(8,128)(2,1)S(1)}, u32[]{:S(2)}, u32[]{:S(2)}) collective-permute-start(bf16[2,32,2560]{2,1,0:T(8,128)(2,1)S(1)} %collective-permute-done.9.refs_1_), channel_id=1, source_target_pairs={{0,240},{16,0},{32,16},{48,32},{64,48},{80,64},{96,80},{112,96},{1... | collective-permute-start | bytes 983048 | tf_op jit(solution)/shard_map/ppermute | solution.py:159
  102.2 5.2 %collective-permute-start.16 = (bf16[2,32,2560]{2,1,0:T(8,128)(2,1)S(1)}, bf16[2,32,2560]{2,1,0:T(8,128)(2,1)S(1)}, u32[]{:S(2)}, u32[]{:S(2)}) collective-permute-start(bf16[2,32,2560]{2,1,0:T(8,128)(2,1)S(1)} %collective-permute-done.12.refs_4_), channel_id=1, source_target_pairs={{0,240},{16,0},{32,16},{48,32},{64,48},{80,64},{96,80},{112,96},{1... | collective-permute-start | bytes 983048 | tf_op jit(solution)/shard_map/ppermute | solution.py:159
  110.8 5.2 %collective-permute-start.17 = (bf16[2,32,2560]{2,1,0:T(8,128)(2,1)S(1)}, bf16[2,32,2560]{2,1,0:T(8,128)(2,1)S(1)}, u32[]{:S(2)}, u32[]{:S(2)}) collective-permute-start(bf16[2,32,2560]{2,1,0:T(8,128)(2,1)S(1)} %collective-permute-done.13.refs_5_), channel_id=1, source_target_pairs={{0,240},{16,0},{32,16},{48,32},{64,48},{80,64},{96,80},{112,96},{1... | collective-permute-start | bytes 983048 | tf_op jit(solution)/shard_map/ppermute | solution.py:159
  119.4 5.2 %collective-permute-start.20 = (bf16[2,32,2560]{2,1,0:T(8,128)(2,1)S(1)}, bf16[2,32,2560]{2,1,0:T(8,128)(2,1)S(1)}, u32[]{:S(2)}, u32[]{:S(2)}) collective-permute-start(bf16[2,32,2560]{2,1,0:T(8,128)(2,1)S(1)} %collective-permute-done.16.refs_8_), channel_id=1, source_target_pairs={{0,240},{16,0},{32,16},{48,32},{64,48},{80,64},{96,80},{112,96},{1... | collective-permute-start | bytes 983048 | tf_op jit(solution)/shard_map/ppermute | solution.py:159
  128.0 5.2 %collective-permute-start.21 = (bf16[2,32,2560]{2,1,0:T(8,128)(2,1)S(1)}, bf16[2,32,2560]{2,1,0:T(8,128)(2,1)}, u32[]{:S(2)}, u32[]{:S(2)}) collective-permute-start(bf16[2,32,2560]{2,1,0:T(8,128)(2,1)S(1)} %collective-permute-done.17.refs_9_), channel_id=1, source_target_pairs={{0,240},{16,0},{32,16},{48,32},{64,48},{80,64},{96,80},{112,96},{1... | collective-permute-start | bytes 983048 | tf_op jit(solution)/shard_map/ppermute | solution.py:159
  136.5 5.2 %collective-permute-start.24 = (bf16[2,32,2560]{2,1,0:T(8,128)(2,1)S(1)}, bf16[2,32,2560]{2,1,0:T(8,128)(2,1)}, u32[]{:S(2)}, u32[]{:S(2)}) collective-permute-start(bf16[2,32,2560]{2,1,0:T(8,128)(2,1)S(1)} %collective-permute-done.20.refs_0_), channel_id=1, source_target_pairs={{0,240},{16,0},{32,16},{48,32},{64,48},{80,64},{96,80},{112,96},{1... | collective-permute-start | bytes 983048 | tf_op jit(solution)/shard_map/ppermute | solution.py:159
  145.1 5.2 %collective-permute-start.25 = (bf16[2,32,2560]{2,1,0:T(8,128)(2,1)}, bf16[2,32,2560]{2,1,0:T(8,128)(2,1)}, u32[]{:S(2)}, u32[]{:S(2)}) collective-permute-start(bf16[2,32,2560]{2,1,0:T(8,128)(2,1)} %collective-permute-done.21.refs_1_), channel_id=1, source_target_pairs={{0,240},{16,0},{32,16},{48,32},{64,48},{80,64},{96,80},{112,96},{1... | collective-permute-start | bytes 983048 | tf_op jit(solution)/shard_map/ppermute | solution.py:159
  150.3 2.0 collective-permute-start.26
  152.3 5.2 %collective-permute-start.28 = (bf16[2,32,2560]{2,1,0:T(8,128)(2,1)}, bf16[2,32,2560]{2,1,0:T(8,128)(2,1)}, u32[]{:S(2)}, u32[]{:S(2)}) collective-permute-start(bf16[2,32,2560]{2,1,0:T(8,128)(2,1)} %collective-permute-done.24.refs_4_), channel_id=1, source_target_pairs={{0,240},{16,0},{32,16},{48,32},{64,48},{80,64},{96,80},{112,96},{1... | collective-permute-start | bytes 983048 | tf_op jit(solution)/shard_map/ppermute | solution.py:159
  157.5 2.0 collective-permute-start.29
  164.9 2.6 %product.5.refs_2_ = f32[4,96,128]{2,1,0:T(8,128)S(1)} custom-call(bf16[192,2560]{1,0:T(8,128)(2,1)S(1)} %order.2.right, bf16[2,32,2560]{2,1,0:T(8,128)(2,1)S(1)} %copy-done.32, bf16[2,32,2560]{2,1,0:T(8,128)(2,1)} %collective-permute-done.21.refs_1_, bf16[2,32,2560]{2,1,0:T(8,128)(2,1)} %collective-permute-done.22.refs_2_, ...), custom_call_target="tpu_custom_call" | custom-call | tf_op jit(solution)/shard_map/product/pallas_call | solution.py:64
  168.0 2.7 %assemble.1 = f32[8,96,256]{2,1,0:T(8,128)} custom-call(s32[1]{0:T(128)} %bitcast.place, bf16[192,2560]{1,0:T(8,128)(2,1)S(1)} %order.2.right, f32[5,96,128]{2,1,0:T(8,128)S(1)} %product.3.refs_0_, f32[6,96,128]{2,1,0:T(8,128)S(1)} %product.4.refs_1_, f32[4,96,128]{2,1,0:T(8,128)S(1)} %product.5.refs_2_, ...), custom_call_target="tpu_custom_call" | custom-call | tf_op jit(solution)/shard_map/assemble/pallas_call | solution.py:92
  170.7 7.3 %all-to-all-start = ((f32[8,96,256]{2,1,0:T(8,128)}), f32[8,96,256]{2,1,0:T(8,128)S(1)}, u32[]{:S(2)}, u32[]{:S(2)}) async-start(f32[8,96,256]{2,1,0:T(8,128)} %assemble.1), calls=%async_computation | async-start | bytes 1572864 | tf_op jit(solution)/shard_map/all_to_all | solution.py:168
  178.7 16.2 %all-to-all-done.refs_0_ = f32[8,96,256]{2,1,0:T(8,128)S(1)} async-done(((f32[8,96,256]{2,1,0:T(8,128)}), f32[8,96,256]{2,1,0:T(8,128)S(1)}, u32[]{:S(2)}, u32[]{:S(2)}) %all-to-all-start) | async-done | bytes 786464 | tf_op jit(solution)/shard_map/all_to_all | solution.py:168
  (119 shorter events, 40.1 us)
Async XLA Ops:
  1.2 53.1 %collective-permute-start = (bf16[2,32,2560]{2,1,0:T(8,128)(2,1)S(1)}, bf16[2,32,2560]{2,1,0:T(8,128)(2,1)S(1)}, u32[]{:S(2)}, u32[]{:S(2)}) collective-permute-start(bf16[2,32,2560]{2,1,0:T(8,128)(2,1)S(1)} %get-tuple-element.6.refs_0_), channel_id=1, source_target_pairs={{0,240},{16,0},{32,16},{48,32},{64,48},{80,64},{96,80},{112,96},{1... | collective-permute-start | bytes 983048 | tf_op jit(solution)/shard_map/ppermute | solution.py:159
  61.5 15.0 %collective-permute-start.5 = (bf16[2,32,2560]{2,1,0:T(8,128)(2,1)S(1)}, bf16[2,32,2560]{2,1,0:T(8,128)(2,1)S(1)}, u32[]{:S(2)}, u32[]{:S(2)}) collective-permute-start(bf16[2,32,2560]{2,1,0:T(8,128)(2,1)S(1)} %collective-permute-done.1.refs_3_), channel_id=1, source_target_pairs={{0,240},{16,0},{32,16},{48,32},{64,48},{80,64},{96,80},{112,96},{1... | collective-permute-start | bytes 983048 | tf_op jit(solution)/shard_map/ppermute | solution.py:159
  66.7 15.7 %collective-permute-start.6 = (bf16[2,32,2560]{2,1,0:T(8,128)(2,1)S(1)}, bf16[2,32,2560]{2,1,0:T(8,128)(2,1)S(1)}, u32[]{:S(2)}, u32[]{:S(2)}) collective-permute-start(bf16[2,32,2560]{2,1,0:T(8,128)(2,1)S(1)} %collective-permute-done.2.refs_4_), channel_id=1, source_target_pairs={{0,16},{16,32},{32,48},{48,64},{64,80},{80,96},{96,112},{112,128},... | collective-permute-start | bytes 983048 | tf_op jit(solution)/shard_map/ppermute | solution.py:161
  68.6 16.5 %collective-permute-start.8 = (bf16[2,32,2560]{2,1,0:T(8,128)(2,1)S(1)}, bf16[2,32,2560]{2,1,0:T(8,128)(2,1)S(1)}, u32[]{:S(2)}, u32[]{:S(2)}) collective-permute-start(bf16[2,32,2560]{2,1,0:T(8,128)(2,1)S(1)} %collective-permute-done.4.refs_6_), channel_id=1, source_target_pairs={{0,240},{16,0},{32,16},{48,32},{64,48},{80,64},{96,80},{112,96},{1... | collective-permute-start | bytes 983048 | tf_op jit(solution)/shard_map/ppermute | solution.py:159
  73.8 17.1 %collective-permute-start.11 = (bf16[2,32,2560]{2,1,0:T(8,128)(2,1)S(1)}, bf16[2,32,2560]{2,1,0:T(8,128)(2,1)S(1)}, u32[]{:S(2)}, u32[]{:S(2)}) collective-permute-start(bf16[2,32,2560]{2,1,0:T(8,128)(2,1)S(1)} %collective-permute-done.7.refs_9_), channel_id=1, source_target_pairs={{0,16},{16,32},{32,48},{48,64},{64,80},{80,96},{96,112},{112,128},... | collective-permute-start | bytes 983048 | tf_op jit(solution)/shard_map/ppermute | solution.py:161
  76.5 17.1 %collective-permute-start.9 = (bf16[2,32,2560]{2,1,0:T(8,128)(2,1)S(1)}, bf16[2,32,2560]{2,1,0:T(8,128)(2,1)S(1)}, u32[]{:S(2)}, u32[]{:S(2)}) collective-permute-start(bf16[2,32,2560]{2,1,0:T(8,128)(2,1)S(1)} %collective-permute-done.5.refs_7_), channel_id=1, source_target_pairs={{0,240},{16,0},{32,16},{48,32},{64,48},{80,64},{96,80},{112,96},{1... | collective-permute-start | bytes 983048 | tf_op jit(solution)/shard_map/ppermute | solution.py:159
  82.4 17.1 %collective-permute-start.10 = (bf16[2,32,2560]{2,1,0:T(8,128)(2,1)S(1)}, bf16[2,32,2560]{2,1,0:T(8,128)(2,1)S(1)}, u32[]{:S(2)}, u32[]{:S(2)}) collective-permute-start(bf16[2,32,2560]{2,1,0:T(8,128)(2,1)S(1)} %collective-permute-done.6.refs_8_), channel_id=1, source_target_pairs={{0,16},{16,32},{32,48},{48,64},{64,80},{80,96},{96,112},{112,128},... | collective-permute-start | bytes 983048 | tf_op jit(solution)/shard_map/ppermute | solution.py:161
  85.1 17.1 %collective-permute-start.12 = (bf16[2,32,2560]{2,1,0:T(8,128)(2,1)S(1)}, bf16[2,32,2560]{2,1,0:T(8,128)(2,1)S(1)}, u32[]{:S(2)}, u32[]{:S(2)}) collective-permute-start(bf16[2,32,2560]{2,1,0:T(8,128)(2,1)S(1)} %collective-permute-done.8.refs_0_), channel_id=1, source_target_pairs={{0,240},{16,0},{32,16},{48,32},{64,48},{80,64},{96,80},{112,96},{1... | collective-permute-start | bytes 983048 | tf_op jit(solution)/shard_map/ppermute | solution.py:159
  91.0 17.1 %collective-permute-start.15 = (bf16[2,32,2560]{2,1,0:T(8,128)(2,1)S(1)}, bf16[2,32,2560]{2,1,0:T(8,128)(2,1)S(1)}, u32[]{:S(2)}, u32[]{:S(2)}) collective-permute-start(bf16[2,32,2560]{2,1,0:T(8,128)(2,1)S(1)} %collective-permute-done.11.refs_3_), channel_id=1, source_target_pairs={{0,16},{16,32},{32,48},{48,64},{64,80},{80,96},{96,112},{112,128},... | collective-permute-start | bytes 983048 | tf_op jit(solution)/shard_map/ppermute | solution.py:161
  93.6 17.2 %collective-permute-start.13 = (bf16[2,32,2560]{2,1,0:T(8,128)(2,1)S(1)}, bf16[2,32,2560]{2,1,0:T(8,128)(2,1)S(1)}, u32[]{:S(2)}, u32[]{:S(2)}) collective-permute-start(bf16[2,32,2560]{2,1,0:T(8,128)(2,1)S(1)} %collective-permute-done.9.refs_1_), channel_id=1, source_target_pairs={{0,240},{16,0},{32,16},{48,32},{64,48},{80,64},{96,80},{112,96},{1... | collective-permute-start | bytes 983048 | tf_op jit(solution)/shard_map/ppermute | solution.py:159
  99.5 17.2 %collective-permute-start.14 = (bf16[2,32,2560]{2,1,0:T(8,128)(2,1)S(1)}, bf16[2,32,2560]{2,1,0:T(8,128)(2,1)S(1)}, u32[]{:S(2)}, u32[]{:S(2)}) collective-permute-start(bf16[2,32,2560]{2,1,0:T(8,128)(2,1)S(1)} %collective-permute-done.10.refs_2_), channel_id=1, source_target_pairs={{0,16},{16,32},{32,48},{48,64},{64,80},{80,96},{96,112},{112,128},... | collective-permute-start | bytes 983048 | tf_op jit(solution)/shard_map/ppermute | solution.py:161
  102.2 17.1 %collective-permute-start.16 = (bf16[2,32,2560]{2,1,0:T(8,128)(2,1)S(1)}, bf16[2,32,2560]{2,1,0:T(8,128)(2,1)S(1)}, u32[]{:S(2)}, u32[]{:S(2)}) collective-permute-start(bf16[2,32,2560]{2,1,0:T(8,128)(2,1)S(1)} %collective-permute-done.12.refs_4_), channel_id=1, source_target_pairs={{0,240},{16,0},{32,16},{48,32},{64,48},{80,64},{96,80},{112,96},{1... | collective-permute-start | bytes 983048 | tf_op jit(solution)/shard_map/ppermute | solution.py:159
  108.1 17.1 %collective-permute-start.19 = (bf16[2,32,2560]{2,1,0:T(8,128)(2,1)S(1)}, bf16[2,32,2560]{2,1,0:T(8,128)(2,1)S(1)}, u32[]{:S(2)}, u32[]{:S(2)}) collective-permute-start(bf16[2,32,2560]{2,1,0:T(8,128)(2,1)S(1)} %collective-permute-done.15.refs_7_), channel_id=1, source_target_pairs={{0,16},{16,32},{32,48},{48,64},{64,80},{80,96},{96,112},{112,128},... | collective-permute-start | bytes 983048 | tf_op jit(solution)/shard_map/ppermute | solution.py:161
  110.8 17.2 %collective-permute-start.17 = (bf16[2,32,2560]{2,1,0:T(8,128)(2,1)S(1)}, bf16[2,32,2560]{2,1,0:T(8,128)(2,1)S(1)}, u32[]{:S(2)}, u32[]{:S(2)}) collective-permute-start(bf16[2,32,2560]{2,1,0:T(8,128)(2,1)S(1)} %collective-permute-done.13.refs_5_), channel_id=1, source_target_pairs={{0,240},{16,0},{32,16},{48,32},{64,48},{80,64},{96,80},{112,96},{1... | collective-permute-start | bytes 983048 | tf_op jit(solution)/shard_map/ppermute | solution.py:159
  116.7 17.1 %collective-permute-start.18 = (bf16[2,32,2560]{2,1,0:T(8,128)(2,1)S(1)}, bf16[2,32,2560]{2,1,0:T(8,128)(2,1)S(1)}, u32[]{:S(2)}, u32[]{:S(2)}) collective-permute-start(bf16[2,32,2560]{2,1,0:T(8,128)(2,1)S(1)} %collective-permute-done.14.refs_6_), channel_id=1, source_target_pairs={{0,16},{16,32},{32,48},{48,64},{64,80},{80,96},{96,112},{112,128},... | collective-permute-start | bytes 983048 | tf_op jit(solution)/shard_map/ppermute | solution.py:161
  119.4 17.2 %collective-permute-start.20 = (bf16[2,32,2560]{2,1,0:T(8,128)(2,1)S(1)}, bf16[2,32,2560]{2,1,0:T(8,128)(2,1)S(1)}, u32[]{:S(2)}, u32[]{:S(2)}) collective-permute-start(bf16[2,32,2560]{2,1,0:T(8,128)(2,1)S(1)} %collective-permute-done.16.refs_8_), channel_id=1, source_target_pairs={{0,240},{16,0},{32,16},{48,32},{64,48},{80,64},{96,80},{112,96},{1... | collective-permute-start | bytes 983048 | tf_op jit(solution)/shard_map/ppermute | solution.py:159
  125.3 17.2 %collective-permute-start.23 = (bf16[2,32,2560]{2,1,0:T(8,128)(2,1)S(1)}, bf16[2,32,2560]{2,1,0:T(8,128)(2,1)S(1)}, u32[]{:S(2)}, u32[]{:S(2)}) collective-permute-start(bf16[2,32,2560]{2,1,0:T(8,128)(2,1)S(1)} %collective-permute-done.19.refs_11_), channel_id=1, source_target_pairs={{0,16},{16,32},{32,48},{48,64},{64,80},{80,96},{96,112},{112,128},... | collective-permute-start | bytes 983048 | tf_op jit(solution)/shard_map/ppermute | solution.py:161
  128.0 17.2 %collective-permute-start.21 = (bf16[2,32,2560]{2,1,0:T(8,128)(2,1)S(1)}, bf16[2,32,2560]{2,1,0:T(8,128)(2,1)}, u32[]{:S(2)}, u32[]{:S(2)}) collective-permute-start(bf16[2,32,2560]{2,1,0:T(8,128)(2,1)S(1)} %collective-permute-done.17.refs_9_), channel_id=1, source_target_pairs={{0,240},{16,0},{32,16},{48,32},{64,48},{80,64},{96,80},{112,96},{1... | collective-permute-start | bytes 983048 | tf_op jit(solution)/shard_map/ppermute | solution.py:159
  133.8 16.4 %collective-permute-start.22 = (bf16[2,32,2560]{2,1,0:T(8,128)(2,1)S(1)}, bf16[2,32,2560]{2,1,0:T(8,128)(2,1)}, u32[]{:S(2)}, u32[]{:S(2)}) collective-permute-start(bf16[2,32,2560]{2,1,0:T(8,128)(2,1)S(1)} %collective-permute-done.18.refs_10_), channel_id=1, source_target_pairs={{0,16},{16,32},{32,48},{48,64},{64,80},{80,96},{96,112},{112,128},... | collective-permute-start | bytes 983048 | tf_op jit(solution)/shard_map/ppermute | solution.py:161
  136.5 15.7 %collective-permute-start.24 = (bf16[2,32,2560]{2,1,0:T(8,128)(2,1)S(1)}, bf16[2,32,2560]{2,1,0:T(8,128)(2,1)}, u32[]{:S(2)}, u32[]{:S(2)}) collective-permute-start(bf16[2,32,2560]{2,1,0:T(8,128)(2,1)S(1)} %collective-permute-done.20.refs_0_), channel_id=1, source_target_pairs={{0,240},{16,0},{32,16},{48,32},{64,48},{80,64},{96,80},{112,96},{1... | collective-permute-start | bytes 983048 | tf_op jit(solution)/shard_map/ppermute | solution.py:159
  142.4 15.0 %collective-permute-start.27 = (bf16[2,32,2560]{2,1,0:T(8,128)(2,1)S(1)}, bf16[2,32,2560]{2,1,0:T(8,128)(2,1)}, u32[]{:S(2)}, u32[]{:S(2)}) collective-permute-start(bf16[2,32,2560]{2,1,0:T(8,128)(2,1)S(1)} %collective-permute-done.23.refs_3_), channel_id=1, source_target_pairs={{0,16},{16,32},{32,48},{48,64},{64,80},{80,96},{96,112},{112,128},... | collective-permute-start | bytes 983048 | tf_op jit(solution)/shard_map/ppermute | solution.py:161
  145.1 19.7 %collective-permute-start.25 = (bf16[2,32,2560]{2,1,0:T(8,128)(2,1)}, bf16[2,32,2560]{2,1,0:T(8,128)(2,1)}, u32[]{:S(2)}, u32[]{:S(2)}) collective-permute-start(bf16[2,32,2560]{2,1,0:T(8,128)(2,1)} %collective-permute-done.21.refs_1_), channel_id=1, source_target_pairs={{0,240},{16,0},{32,16},{48,32},{64,48},{80,64},{96,80},{112,96},{1... | collective-permute-start | bytes 983048 | tf_op jit(solution)/shard_map/ppermute | solution.py:159
  152.3 15.2 %collective-permute-start.28 = (bf16[2,32,2560]{2,1,0:T(8,128)(2,1)}, bf16[2,32,2560]{2,1,0:T(8,128)(2,1)}, u32[]{:S(2)}, u32[]{:S(2)}) collective-permute-start(bf16[2,32,2560]{2,1,0:T(8,128)(2,1)} %collective-permute-done.24.refs_4_), channel_id=1, source_target_pairs={{0,240},{16,0},{32,16},{48,32},{64,48},{80,64},{96,80},{112,96},{1... | collective-permute-start | bytes 983048 | tf_op jit(solution)/shard_map/ppermute | solution.py:159
  170.7 24.1 %all-to-all-start = ((f32[8,96,256]{2,1,0:T(8,128)}), f32[8,96,256]{2,1,0:T(8,128)S(1)}, u32[]{:S(2)}, u32[]{:S(2)}) async-start(f32[8,96,256]{2,1,0:T(8,128)} %assemble.1), calls=%async_computation | async-start | bytes 1572864 | tf_op jit(solution)/shard_map/all_to_all | solution.py:168
  (44 other events, 311.9 us)
